TPU v7x, 32 devices: a whole 2x2x4 slice. The times are simulated.
32 devices in a mesh: tm: 4 (over x, core), space: 8 (over z, y).
Axes of the slice: x: 2, y: 2, z: 4, core: 2. Of those that a mesh axis runs over, the one named last changes fastest.
Arguments:
- span_opening: float32 [4, 32, 64, 128], P('tm', 'space'), may hold values from -8 to 8
- source_power: float32 [4, 2, 32, 64, 128], P('tm', None, 'space'), may hold values from -24 to 24
- warmth_retention: float32 [32, 64, 128], P('space'), may hold values from 0.02 to 0.4
Outputs:
- fpoint: float32 [4, 32, 64, 128], P('tm', 'space')
- updated: float32 [4, 32, 64, 128], P('tm', 'space')
All inputs are finite; a program needn't handle non-finite values.
Results may differ from a plain program's by a relative error of at most 0.0001.
Values sent between devices are 32-bit elements; how exact they have to be, the bound alone decides.
A program may use at most 64 MiB of HBM per device.

v0:
```python
import jax
import jax.numpy as jnp
from jax import lax
from jax.sharding import PartitionSpec as P

COARSE_SWEEPS = 24


relax_weight = 0.8


def with_halo(cells, sides, width):
    for axis, dim in sides:
        count = lax.axis_size(axis)
        ends = count - 1
        head = lax.slice_in_dim(cells, 0, width, axis=dim)
        tail = lax.slice_in_dim(cells, cells.shape[dim] - width, cells.shape[dim], axis=dim)
        cells = jnp.concatenate(
            [
                lax.ppermute(tail, axis, [(i, (i + 1) % count) for i in range(ends)]),
                cells,
                lax.ppermute(head, axis, [((i + 1) % count, i) for i in range(ends)]),
            ],
            axis=dim,
        )
    return cells


def passed_along(x, axis, by):
    peers = lax.axis_size(axis)
    pairs = [(i, i + by) for i in range(peers) if 0 <= i + by < peers]
    return lax.ppermute(x, axis, pairs)


def mean_to_rougher(field):
    extent_layout = field.shape
    blocks = field.reshape(
        extent_layout[0] // 2, 2, extent_layout[1] // 2, 2, extent_layout[2] // 2, 2
    )
    return blocks.mean(axis=(1, 3, 5))


def lift_to_finer(field):
    extent_layout = field.shape
    grown = jnp.broadcast_to(
        field[:, None, :, None, :, None],
        (extent_layout[0], 2, extent_layout[1], 2, extent_layout[2], 2),
    )
    return grown.reshape(2 * extent_layout[0], 2 * extent_layout[1], 2 * extent_layout[2])


def neighbour_sum(field, padded):
    flat = jnp.pad(field, ((0, 0), (1, 1), (1, 1)))
    total = padded[2:] + padded[:-2]
    total = total + flat[:, 2:, 1:-1] + flat[:, :-2, 1:-1]
    return total + flat[:, 1:-1, 2:] + flat[:, 1:-1, :-2]


def apply_nearby_part(field, retention_quantities, conductance):
    padded = jnp.pad(field, ((1, 1), (0, 0), (0, 0)))
    return (retention_quantities + 6.0 * conductance) * field - conductance * neighbour_sum(
        field, padded
    )


def apply_split(field, retention_quantities, conductance):
    padded = with_halo(field, (("space", 0),), 1)
    return (retention_quantities + 6.0 * conductance) * field - conductance * neighbour_sum(
        field, padded
    )


def assemble(gathered, teams_across, fragments):
    depth = gathered.shape[0] // fragments
    rows, cols = (gathered.shape[1], gathered.shape[2])
    blocks = gathered.reshape(fragments // teams_across, teams_across, depth, rows, cols)
    blocks = jnp.transpose(blocks, (0, 2, 1, 3, 4))
    return blocks.reshape(fragments // teams_across * depth, teams_across * rows, cols)


def pull_out(whole, teams_across, location, depth):
    plane_start = location // teams_across * depth
    part_block = lax.dynamic_slice_in_dim(whole, plane_start, depth, 0)
    return part_block


def bottom_grid_inversion(load_components, retention_quantities):
    conductance = 0.125
    diagonal = retention_quantities + 6.0 * conductance
    first_approximation = relax_weight * load_components / diagonal
    for sweep_index in range(COARSE_SWEEPS - 1):
        first_approximation = (
            first_approximation
            + relax_weight
            * (
                load_components
                - apply_nearby_part(first_approximation, retention_quantities, conductance)
            )
            / diagonal
        )
    return first_approximation


def personal_hierarchy_cycle(load_components, volume_holdings, hierarchy_layers):
    if hierarchy_layers == 3:
        return bottom_grid_inversion(load_components, volume_holdings[3])
    conductance = 0.5**hierarchy_layers
    retention_quantities = volume_holdings[hierarchy_layers]
    diagonal = retention_quantities + 6.0 * conductance
    first_approximation = relax_weight * load_components / diagonal
    first_approximation = (
        first_approximation
        + relax_weight
        * (
            load_components
            - apply_nearby_part(first_approximation, retention_quantities, conductance)
        )
        / diagonal
    )
    further_moments = load_components - apply_nearby_part(
        first_approximation, retention_quantities, conductance
    )
    first_approximation = first_approximation + lift_to_finer(
        personal_hierarchy_cycle(
            mean_to_rougher(further_moments), volume_holdings, hierarchy_layers + 1
        )
    )
    for sweep_index in range(2):
        first_approximation = (
            first_approximation
            + relax_weight
            * (
                load_components
                - apply_nearby_part(first_approximation, retention_quantities, conductance)
            )
            / diagonal
        )
    return first_approximation


def round_division(
    load_components,
    local_caps,
    whole_caps,
    hierarchy_layers,
    location,
    system_matrix,
    teams_across,
    fragments,
):
    conductance = 0.5**hierarchy_layers
    retention_quantities = local_caps[hierarchy_layers]
    diagonal = retention_quantities + 6.0 * conductance
    first_approximation = relax_weight * load_components / diagonal
    first_approximation = (
        first_approximation
        + relax_weight
        * (load_components - system_matrix(first_approximation, retention_quantities, conductance))
        / diagonal
    )
    further_moments = load_components - system_matrix(
        first_approximation, retention_quantities, conductance
    )
    lower_side = mean_to_rougher(further_moments)
    whole_side = assemble(
        lax.all_gather(lower_side, "space", axis=0, tiled=True), teams_across, fragments
    )
    complete_adjustment = personal_hierarchy_cycle(whole_side, whole_caps, hierarchy_layers + 1)
    own_fix = pull_out(complete_adjustment, teams_across, location, lower_side.shape[0])
    adjustment = lift_to_finer(own_fix)
    first_approximation = first_approximation + adjustment
    for sweep_index in range(2):
        first_approximation = (
            first_approximation
            + relax_weight
            * (
                load_components
                - system_matrix(first_approximation, retention_quantities, conductance)
            )
            / diagonal
        )
    return first_approximation


def shards(span_opening, source_power, warmth_retention):
    location = lax.axis_index("space")
    fragments = lax.axis_size("space")
    step_count = source_power.shape[1]
    launch_condition = span_opening[0]
    injections = source_power[0]
    teams_across = 1
    mid_cap = mean_to_rougher(warmth_retention)
    whole_mid = assemble(
        lax.all_gather(mid_cap, "space", axis=0, tiled=True), teams_across, fragments
    )
    whole_low = mean_to_rougher(whole_mid)
    whole_caps = [None, whole_mid, whole_low, mean_to_rougher(whole_low)]
    local_caps = [warmth_retention, mid_cap]
    warmth_distribution = launch_condition
    opening_condition = warmth_distribution
    for moment_count in range(step_count):
        load_components = warmth_retention * warmth_distribution + injections[moment_count]
        warmth_distribution = round_division(
            load_components,
            local_caps,
            whole_caps,
            0,
            location,
            apply_split,
            teams_across,
            fragments,
        )
        if moment_count == 0:
            opening_condition = warmth_distribution
    shifted_over = passed_along(warmth_distribution, "tm", 1)
    updated = jnp.where(lax.axis_index("tm") == 0, launch_condition, shifted_over)
    return (opening_condition[None], updated[None])


def solution(mesh):
    in_specs = (
        P("tm", "space", None, None),
        P("tm", None, "space", None, None),
        P("space", None, None),
    )
    out_specs = (P("tm", "space", None, None), P("tm", "space", None, None))
    return jax.shard_map(shards, mesh=mesh, in_specs=in_specs, out_specs=out_specs, check_vma=False)
```

profile of v0, /device:TPU:10, one launch (start us, length us, event | category | flops | bytes accessed | tf_op | source)
XLA Modules:
  0.0 309.6 jit_solution(8340510009194880317)
XLA Ops:
  0.6 1.1 multiply_divide_fusion.3
  1.7 3.3 %collective-permute-start = (f32[1,64,128]{2,1,0:T(8,128)S(1)}, f32[1,64,128]{2,1,0:T(8,128)S(1)}, u32[]{:S(2)}, u32[]{:S(2)}) collective-permute-start(f32[1,64,128]{2,1,0:T(8,128)S(1)} %get-tuple-element.23), channel_id=1, source_target_pairs={{1,0},{2,1},{3,2},{4,3},{5,4},{6,5},{7,6},{9,8},{10,9},{11,10},{12... | collective-permute-start | bytes 98312 | tf_op jit(solution)/shard_map/ppermute | solution.py:22
  5.0 2.7 collective-permute-start.1
  7.7 10.5 %reshape.58 = f32[2,2,32,2,64,2]{5,4,3,2,1,0:T(8,128)} reshape(f32[4,64,128]{2,1,0:T(8,128)} %param.5) | data formatting | bytes 262144 | tf_op jit(solution)/shard_map/reshape | solution.py:37
  18.2 4.0 %reduce_sum.82 = f32[2,32,64]{2,1,0:T(8,128)S(1)} reduce(f32[2,2,32,2,64,2]{5,4,3,2,1,0:T(8,128)} %reshape.58, f32[]{:T(128)} %constant.53.clone.1), dimensions={1,3,5}, to_apply=%region_1.0 | reduce | flops 28672 | bytes 147460 | tf_op jit(solution)/shard_map/reduce_sum | solution.py:40
  22.4 4.2 %collective-permute-start.2 = (f32[1,64,128]{2,1,0:T(8,128)S(1)}, f32[1,64,128]{2,1,0:T(8,128)S(1)}, u32[]{:S(2)}, u32[]{:S(2)}) collective-permute-start(f32[1,64,128]{2,1,0:T(8,128)S(1)} %get-tuple-element.21), channel_id=1, source_target_pairs={{1,0},{2,1},{3,2},{4,3},{5,4},{6,5},{7,6},{9,8},{10,9},{11,10},{12... | collective-permute-start | bytes 98312 | tf_op jit(solution)/shard_map/ppermute | solution.py:22
  26.7 2.0 collective-permute-start.3
  28.7 28.2 %all_gather.10 = f32[16,32,64]{2,1,0:T(8,128)S(1)} all-gather(f32[2,32,64]{2,1,0:T(8,128)S(1)} %broadcast_multiply_fusion.2), channel_id=1, replica_groups=mesh['tm'=4,'space'=8] {'space'}, dimensions={0}, use_global_device_ids=true | all-gather | bytes 147456 | tf_op jit(solution)/shard_map/all_gather | solution.py:194
  56.9 10.0 %reshape_reshape_transpose_reshape.3 = f32[8,2,16,2,32,2]{5,4,3,2,1,0:T(8,128)} reshape(f32[16,32,64]{2,1,0:T(8,128)S(1)} %all_gather.10) | data formatting | bytes 262144 | tf_op jit(solution)/shard_map/reshape;reshape;transpose;reshape | solution.py:37
  66.9 4.1 %reduce_sum.84 = f32[8,16,32]{2,1,0:T(8,128)S(1)} reduce(f32[8,2,16,2,32,2]{5,4,3,2,1,0:T(8,128)} %reshape_reshape_transpose_reshape.3, f32[]{:T(128)} %constant.53.clone.1), dimensions={1,3,5}, to_apply=%region_3.4 | reduce | flops 28672 | bytes 147460 | tf_op jit(solution)/shard_map/reduce_sum | solution.py:40
  71.1 9.8 %reshape.57 = f32[2,2,32,2,64,2]{5,4,3,2,1,0:T(8,128)} reshape(f32[4,64,128]{2,1,0:T(8,128)S(1)} %fusion.84) | data formatting | bytes 262144 | tf_op jit(solution)/shard_map/reshape | solution.py:37
  80.9 4.0 %reduce_sum.81 = f32[2,32,64]{2,1,0:T(8,128)S(1)} reduce(f32[2,2,32,2,64,2]{5,4,3,2,1,0:T(8,128)} %reshape.57, f32[]{:T(128)} %constant.53.clone.1), dimensions={1,3,5}, to_apply=%region_0.0 | reduce | flops 28672 | bytes 147460 | tf_op jit(solution)/shard_map/reduce_sum | solution.py:40
  84.9 30.9 %all_gather.9 = f32[16,32,64]{2,1,0:T(8,128)S(1)} all-gather(f32[2,32,64]{2,1,0:T(8,128)S(1)} %broadcast_multiply_fusion.3), channel_id=1, replica_groups=mesh['tm'=4,'space'=8] {'space'}, dimensions={0}, use_global_device_ids=true | all-gather | bytes 147456 | tf_op jit(solution)/shard_map/all_gather | solution.py:166
  116.3 10.0 %reshape.59 = f32[8,2,16,2,32,2]{5,4,3,2,1,0:T(8,128)} reshape(f32[16,32,64]{2,1,0:T(8,128)S(1)} %fusion.18) | data formatting | bytes 262144 | tf_op jit(solution)/shard_map/reshape | solution.py:37
  126.4 4.1 %reduce_sum.83 = f32[8,16,32]{2,1,0:T(8,128)S(1)} reduce(f32[8,2,16,2,32,2]{5,4,3,2,1,0:T(8,128)} %reshape.59, f32[]{:T(128)} %constant.53.clone.1), dimensions={1,3,5}, to_apply=%region_2.0 | reduce | flops 28672 | bytes 147460 | tf_op jit(solution)/shard_map/reduce_sum | solution.py:40
  135.1 3.9 %broadcast_in_dim.17 = f32[8,2,16,2,32,2]{5,4,3,2,1,0:T(8,128)} broadcast(f32[8,16,32]{2,1,0:T(8,128)S(1)} %fusion.185), dimensions={0,2,4} | broadcast | bytes 147456 | tf_op jit(solution)/shard_map/broadcast_in_dim | solution.py:45
  139.0 8.2 %reshape.62 = f32[16,32,64]{2,1,0:T(8,128)S(1)} reshape(f32[8,2,16,2,32,2]{5,4,3,2,1,0:T(8,128)} %broadcast_in_dim.17) | data formatting | bytes 262144 | tf_op jit(solution)/shard_map/reshape | solution.py:49
  147.7 3.8 %broadcast_in_dim.18 = f32[2,2,32,2,64,2]{5,4,3,2,1,0:T(8,128)} broadcast(f32[2,32,64]{2,1,0:T(8,128)S(1)} %fusion.233), dimensions={0,2,4} | broadcast | bytes 147456 | tf_op jit(solution)/shard_map/broadcast_in_dim | solution.py:45
  151.5 6.9 %reshape.63 = f32[4,64,128]{2,1,0:T(8,128)S(1)} reshape(f32[2,2,32,2,64,2]{5,4,3,2,1,0:T(8,128)} %broadcast_in_dim.18) | data formatting | bytes 262144 | tf_op jit(solution)/shard_map/reshape | solution.py:49
  158.5 4.8 %collective-permute-start.4 = (f32[1,64,128]{2,1,0:T(8,128)S(1)}, f32[1,64,128]{2,1,0:T(8,128)S(1)}, u32[]{:S(2)}, u32[]{:S(2)}) collective-permute-start(f32[1,64,128]{2,1,0:T(8,128)S(1)} %get-tuple-element.19), channel_id=1, source_target_pairs={{1,0},{2,1},{3,2},{4,3},{5,4},{6,5},{7,6},{9,8},{10,9},{11,10},{12... | collective-permute-start | bytes 98312 | tf_op jit(solution)/shard_map/ppermute | solution.py:22
  163.3 1.9 collective-permute-start.5
  165.2 4.8 %collective-permute-done.5 = f32[1,64,128]{2,1,0:T(8,128)S(1)} collective-permute-done((f32[1,64,128]{2,1,0:T(8,128)S(1)}, f32[1,64,128]{2,1,0:T(8,128)S(1)}, u32[]{:S(2)}, u32[]{:S(2)}) %collective-permute-start.5) | collective-permute-done | bytes 32800 | tf_op jit(solution)/shard_map/ppermute | solution.py:20
  170.2 3.0 collective-permute-start.6
  173.2 2.8 collective-permute-start.7
  176.0 3.9 %collective-permute-done.7 = f32[1,64,128]{2,1,0:T(8,128)S(1)} collective-permute-done((f32[1,64,128]{2,1,0:T(8,128)S(1)}, f32[1,64,128]{2,1,0:T(8,128)S(1)}, u32[]{:S(2)}, u32[]{:S(2)}) %collective-permute-start.7) | collective-permute-done | bytes 32800 | tf_op jit(solution)/shard_map/ppermute | solution.py:20
  180.7 1.9 collective-permute-start.8
  182.7 3.9 %collective-permute-start.9 = (f32[1,64,128]{2,1,0:T(8,128)S(1)}, f32[1,64,128]{2,1,0:T(8,128)S(1)}, u32[]{:S(2)}, u32[]{:S(2)}) collective-permute-start(f32[1,64,128]{2,1,0:T(8,128)S(1)} %get-tuple-element.16), channel_id=1, source_target_pairs={{0,1},{1,2},{2,3},{3,4},{4,5},{5,6},{6,7},{8,9},{9,10},{10,11},{11... | collective-permute-start | bytes 98312 | tf_op jit(solution)/shard_map/ppermute | solution.py:20
  186.6 2.8 collective-permute-done.9
  189.5 1.9 collective-permute-start.10
  191.5 4.1 %collective-permute-start.11 = (f32[1,64,128]{2,1,0:T(8,128)S(1)}, f32[1,64,128]{2,1,0:T(8,128)S(1)}, u32[]{:S(2)}, u32[]{:S(2)}) collective-permute-start(f32[1,64,128]{2,1,0:T(8,128)S(1)} %get-tuple-element.14), channel_id=1, source_target_pairs={{0,1},{1,2},{2,3},{3,4},{4,5},{5,6},{6,7},{8,9},{9,10},{10,11},{11... | collective-permute-start | bytes 98312 | tf_op jit(solution)/shard_map/ppermute | solution.py:20
  195.6 2.6 collective-permute-done.11
  198.4 9.8 %reshape.64 = f32[2,2,32,2,64,2]{5,4,3,2,1,0:T(8,128)} reshape(f32[4,64,128]{2,1,0:T(8,128)S(1)} %fusion.117) | data formatting | bytes 262144 | tf_op jit(solution)/shard_map/reshape | solution.py:37
  208.2 4.0 %reduce_sum.87 = f32[2,32,64]{2,1,0:T(8,128)S(1)} reduce(f32[2,2,32,2,64,2]{5,4,3,2,1,0:T(8,128)} %reshape.64, f32[]{:T(128)} %constant.53.clone.1), dimensions={1,3,5}, to_apply=%region_6.7 | reduce | flops 28672 | bytes 147460 | tf_op jit(solution)/shard_map/reduce_sum | solution.py:40
  212.2 27.1 %all_gather.11 = f32[16,32,64]{2,1,0:T(8,128)S(1)} all-gather(f32[2,32,64]{2,1,0:T(8,128)S(1)} %broadcast_multiply_fusion.1), channel_id=1, replica_groups=mesh['tm'=4,'space'=8] {'space'}, dimensions={0}, use_global_device_ids=true | all-gather | bytes 147456 | tf_op jit(solution)/shard_map/all_gather | solution.py:166
  239.9 10.0 %reshape.65 = f32[8,2,16,2,32,2]{5,4,3,2,1,0:T(8,128)} reshape(f32[16,32,64]{2,1,0:T(8,128)S(1)} %fusion.53) | data formatting | bytes 262144 | tf_op jit(solution)/shard_map/reshape | solution.py:37
  249.9 4.1 %reduce_sum.88 = f32[8,16,32]{2,1,0:T(8,128)S(1)} reduce(f32[8,2,16,2,32,2]{5,4,3,2,1,0:T(8,128)} %reshape.65, f32[]{:T(128)} %constant.53.clone.1), dimensions={1,3,5}, to_apply=%region_7.8 | reduce | flops 28672 | bytes 147460 | tf_op jit(solution)/shard_map/reduce_sum | solution.py:40
  257.9 3.9 %broadcast_in_dim.21 = f32[8,2,16,2,32,2]{5,4,3,2,1,0:T(8,128)} broadcast(f32[8,16,32]{2,1,0:T(8,128)S(1)} %fusion.226), dimensions={0,2,4} | broadcast | bytes 147456 | tf_op jit(solution)/shard_map/broadcast_in_dim | solution.py:45
  261.8 8.2 %reshape.68 = f32[16,32,64]{2,1,0:T(8,128)S(1)} reshape(f32[8,2,16,2,32,2]{5,4,3,2,1,0:T(8,128)} %broadcast_in_dim.21) | data formatting | bytes 262144 | tf_op jit(solution)/shard_map/reshape | solution.py:49
  270.5 3.8 %broadcast_in_dim.22 = f32[2,2,32,2,64,2]{5,4,3,2,1,0:T(8,128)} broadcast(f32[2,32,64]{2,1,0:T(8,128)S(1)} %fusion.229), dimensions={0,2,4} | broadcast | bytes 147456 | tf_op jit(solution)/shard_map/broadcast_in_dim | solution.py:45
  274.3 6.9 %reshape.69 = f32[4,64,128]{2,1,0:T(8,128)S(1)} reshape(f32[2,2,32,2,64,2]{5,4,3,2,1,0:T(8,128)} %broadcast_in_dim.22) | data formatting | bytes 262144 | tf_op jit(solution)/shard_map/reshape | solution.py:49
  281.3 4.1 %collective-permute-start.12 = (f32[1,64,128]{2,1,0:T(8,128)S(1)}, f32[1,64,128]{2,1,0:T(8,128)S(1)}, u32[]{:S(2)}, u32[]{:S(2)}) collective-permute-start(f32[1,64,128]{2,1,0:T(8,128)S(1)} %get-tuple-element.11), channel_id=1, source_target_pairs={{1,0},{2,1},{3,2},{4,3},{5,4},{6,5},{7,6},{9,8},{10,9},{11,10},{12... | collective-permute-start | bytes 98312 | tf_op jit(solution)/shard_map/ppermute | solution.py:22
  285.4 1.9 collective-permute-start.13
  287.3 4.8 %collective-permute-done.13 = f32[1,64,128]{2,1,0:T(8,128)S(1)} collective-permute-done((f32[1,64,128]{2,1,0:T(8,128)S(1)}, f32[1,64,128]{2,1,0:T(8,128)S(1)}, u32[]{:S(2)}, u32[]{:S(2)}) %collective-permute-start.13) | collective-permute-done | bytes 32800 | tf_op jit(solution)/shard_map/ppermute | solution.py:20
  292.2 3.6 %collective-permute-start.14 = (f32[1,64,128]{2,1,0:T(8,128)S(1)}, f32[1,64,128]{2,1,0:T(8,128)S(1)}, u32[]{:S(2)}, u32[]{:S(2)}) collective-permute-start(f32[1,64,128]{2,1,0:T(8,128)S(1)} %get-tuple-element.9), channel_id=1, source_target_pairs={{1,0},{2,1},{3,2},{4,3},{5,4},{6,5},{7,6},{9,8},{10,9},{11,10},{12... | collective-permute-start | bytes 98312 | tf_op jit(solution)/shard_map/ppermute | solution.py:22
  295.8 2.3 collective-permute-start.15
  298.1 4.4 %collective-permute-done.15 = f32[1,64,128]{2,1,0:T(8,128)S(1)} collective-permute-done((f32[1,64,128]{2,1,0:T(8,128)S(1)}, f32[1,64,128]{2,1,0:T(8,128)S(1)}, u32[]{:S(2)}, u32[]{:S(2)}) %collective-permute-start.15) | collective-permute-done | bytes 32800 | tf_op jit(solution)/shard_map/ppermute | solution.py:20
  302.7 1.9 collective-permute-start.16
  304.6 4.4 %collective-permute-done.16 = f32[4,64,128]{2,1,0:T(8,128)S(1)} collective-permute-done((f32[4,64,128]{2,1,0:T(8,128)S(1)}, f32[4,64,128]{2,1,0:T(8,128)S(1)}, u32[]{:S(2)}, u32[]{:S(2)}) %collective-permute-start.16) | collective-permute-done | bytes 131104 | tf_op jit(solution)/shard_map/ppermute | solution.py:32
  (122 shorter events, 13.2 us)
Async XLA Ops:
  1.7 20.5 %collective-permute-start = (f32[1,64,128]{2,1,0:T(8,128)S(1)}, f32[1,64,128]{2,1,0:T(8,128)S(1)}, u32[]{:S(2)}, u32[]{:S(2)}) collective-permute-start(f32[1,64,128]{2,1,0:T(8,128)S(1)} %get-tuple-element.23), channel_id=1, source_target_pairs={{1,0},{2,1},{3,2},{4,3},{5,4},{6,5},{7,6},{9,8},{10,9},{11,10},{12... | collective-permute-start | bytes 98312 | tf_op jit(solution)/shard_map/ppermute | solution.py:22
  5.0 17.2 %copy-start = (f32[4,64,128]{2,1,0:T(8,128)S(1)}, f32[4,64,128]{2,1,0:T(8,128)}, u32[]{:S(2)}) copy-start(f32[4,64,128]{2,1,0:T(8,128)} %param.5) | copy-start | bytes 393220
  5.0 17.2 %collective-permute-start.1 = (f32[1,64,128]{2,1,0:T(8,128)S(1)}, f32[1,64,128]{2,1,0:T(8,128)S(1)}, u32[]{:S(2)}, u32[]{:S(2)}) collective-permute-start(f32[1,64,128]{2,1,0:T(8,128)S(1)} %get-tuple-element.24), channel_id=1, source_target_pairs={{0,1},{1,2},{2,3},{3,4},{4,5},{5,6},{6,7},{8,9},{9,10},{10,11},{11... | collective-permute-start | bytes 98312 | tf_op jit(solution)/shard_map/ppermute | solution.py:20
  22.4 48.5 %collective-permute-start.2 = (f32[1,64,128]{2,1,0:T(8,128)S(1)}, f32[1,64,128]{2,1,0:T(8,128)S(1)}, u32[]{:S(2)}, u32[]{:S(2)}) collective-permute-start(f32[1,64,128]{2,1,0:T(8,128)S(1)} %get-tuple-element.21), channel_id=1, source_target_pairs={{1,0},{2,1},{3,2},{4,3},{5,4},{6,5},{7,6},{9,8},{10,9},{11,10},{12... | collective-permute-start | bytes 98312 | tf_op jit(solution)/shard_map/ppermute | solution.py:22
  26.7 44.3 %collective-permute-start.3 = (f32[1,64,128]{2,1,0:T(8,128)S(1)}, f32[1,64,128]{2,1,0:T(8,128)S(1)}, u32[]{:S(2)}, u32[]{:S(2)}) collective-permute-start(f32[1,64,128]{2,1,0:T(8,128)S(1)} %get-tuple-element.22), channel_id=1, source_target_pairs={{0,1},{1,2},{2,3},{3,4},{4,5},{5,6},{6,7},{8,9},{9,10},{10,11},{11... | collective-permute-start | bytes 98312 | tf_op jit(solution)/shard_map/ppermute | solution.py:20
  147.7 32.2 %copy-start.2 = (f32[1,2,4,64,128]{4,3,2,1,0:T(8,128)S(1)}, f32[1,2,4,64,128]{4,3,2,1,0:T(8,128)}, u32[]{:S(2)}) copy-start(f32[1,2,4,64,128]{4,3,2,1,0:T(8,128)} %param.4) | copy-start | bytes 786436
  158.5 6.7 %collective-permute-start.4 = (f32[1,64,128]{2,1,0:T(8,128)S(1)}, f32[1,64,128]{2,1,0:T(8,128)S(1)}, u32[]{:S(2)}, u32[]{:S(2)}) collective-permute-start(f32[1,64,128]{2,1,0:T(8,128)S(1)} %get-tuple-element.19), channel_id=1, source_target_pairs={{1,0},{2,1},{3,2},{4,3},{5,4},{6,5},{7,6},{9,8},{10,9},{11,10},{12... | collective-permute-start | bytes 98312 | tf_op jit(solution)/shard_map/ppermute | solution.py:22
  163.3 6.7 %collective-permute-start.5 = (f32[1,64,128]{2,1,0:T(8,128)S(1)}, f32[1,64,128]{2,1,0:T(8,128)S(1)}, u32[]{:S(2)}, u32[]{:S(2)}) collective-permute-start(f32[1,64,128]{2,1,0:T(8,128)S(1)} %get-tuple-element.20), channel_id=1, source_target_pairs={{0,1},{1,2},{2,3},{3,4},{4,5},{5,6},{6,7},{8,9},{9,10},{10,11},{11... | collective-permute-start | bytes 98312 | tf_op jit(solution)/shard_map/ppermute | solution.py:20
  170.2 5.9 %collective-permute-start.6 = (f32[1,64,128]{2,1,0:T(8,128)S(1)}, f32[1,64,128]{2,1,0:T(8,128)S(1)}, u32[]{:S(2)}, u32[]{:S(2)}) collective-permute-start(f32[1,64,128]{2,1,0:T(8,128)S(1)} %get-tuple-element.17), channel_id=1, source_target_pairs={{1,0},{2,1},{3,2},{4,3},{5,4},{6,5},{7,6},{9,8},{10,9},{11,10},{12... | collective-permute-start | bytes 98312 | tf_op jit(solution)/shard_map/ppermute | solution.py:22
  173.2 6.7 %collective-permute-start.7 = (f32[1,64,128]{2,1,0:T(8,128)S(1)}, f32[1,64,128]{2,1,0:T(8,128)S(1)}, u32[]{:S(2)}, u32[]{:S(2)}) collective-permute-start(f32[1,64,128]{2,1,0:T(8,128)S(1)} %get-tuple-element.18), channel_id=1, source_target_pairs={{0,1},{1,2},{2,3},{3,4},{4,5},{5,6},{6,7},{8,9},{9,10},{10,11},{11... | collective-permute-start | bytes 98312 | tf_op jit(solution)/shard_map/ppermute | solution.py:20
  180.7 5.8 %collective-permute-start.8 = (f32[1,64,128]{2,1,0:T(8,128)S(1)}, f32[1,64,128]{2,1,0:T(8,128)S(1)}, u32[]{:S(2)}, u32[]{:S(2)}) collective-permute-start(f32[1,64,128]{2,1,0:T(8,128)S(1)} %get-tuple-element.15), channel_id=1, source_target_pairs={{1,0},{2,1},{3,2},{4,3},{5,4},{6,5},{7,6},{9,8},{10,9},{11,10},{12... | collective-permute-start | bytes 98312 | tf_op jit(solution)/shard_map/ppermute | solution.py:22
  182.7 6.7 %collective-permute-start.9 = (f32[1,64,128]{2,1,0:T(8,128)S(1)}, f32[1,64,128]{2,1,0:T(8,128)S(1)}, u32[]{:S(2)}, u32[]{:S(2)}) collective-permute-start(f32[1,64,128]{2,1,0:T(8,128)S(1)} %get-tuple-element.16), channel_id=1, source_target_pairs={{0,1},{1,2},{2,3},{3,4},{4,5},{5,6},{6,7},{8,9},{9,10},{10,11},{11... | collective-permute-start | bytes 98312 | tf_op jit(solution)/shard_map/ppermute | solution.py:20
  189.5 6.1 %collective-permute-start.10 = (f32[1,64,128]{2,1,0:T(8,128)S(1)}, f32[1,64,128]{2,1,0:T(8,128)S(1)}, u32[]{:S(2)}, u32[]{:S(2)}) collective-permute-start(f32[1,64,128]{2,1,0:T(8,128)S(1)} %get-tuple-element.13), channel_id=1, source_target_pairs={{1,0},{2,1},{3,2},{4,3},{5,4},{6,5},{7,6},{9,8},{10,9},{11,10},{12... | collective-permute-start | bytes 98312 | tf_op jit(solution)/shard_map/ppermute | solution.py:22
  191.5 6.8 %collective-permute-start.11 = (f32[1,64,128]{2,1,0:T(8,128)S(1)}, f32[1,64,128]{2,1,0:T(8,128)S(1)}, u32[]{:S(2)}, u32[]{:S(2)}) collective-permute-start(f32[1,64,128]{2,1,0:T(8,128)S(1)} %get-tuple-element.14), channel_id=1, source_target_pairs={{0,1},{1,2},{2,3},{3,4},{4,5},{5,6},{6,7},{8,9},{9,10},{10,11},{11... | collective-permute-start | bytes 98312 | tf_op jit(solution)/shard_map/ppermute | solution.py:20
  270.5 38.5 %copy-start.1 = (f32[1,4,64,128]{3,2,1,0:T(8,128)S(1)}, f32[1,4,64,128]{3,2,1,0:T(8,128)}, u32[]{:S(2)}) copy-start(f32[1,4,64,128]{3,2,1,0:T(8,128)} %param.3) | copy-start | bytes 393220
  281.3 6.0 %collective-permute-start.12 = (f32[1,64,128]{2,1,0:T(8,128)S(1)}, f32[1,64,128]{2,1,0:T(8,128)S(1)}, u32[]{:S(2)}, u32[]{:S(2)}) collective-permute-start(f32[1,64,128]{2,1,0:T(8,128)S(1)} %get-tuple-element.11), channel_id=1, source_target_pairs={{1,0},{2,1},{3,2},{4,3},{5,4},{6,5},{7,6},{9,8},{10,9},{11,10},{12... | collective-permute-start | bytes 98312 | tf_op jit(solution)/shard_map/ppermute | solution.py:22
  285.4 6.7 %collective-permute-start.13 = (f32[1,64,128]{2,1,0:T(8,128)S(1)}, f32[1,64,128]{2,1,0:T(8,128)S(1)}, u32[]{:S(2)}, u32[]{:S(2)}) collective-permute-start(f32[1,64,128]{2,1,0:T(8,128)S(1)} %get-tuple-element.12), channel_id=1, source_target_pairs={{0,1},{1,2},{2,3},{3,4},{4,5},{5,6},{6,7},{8,9},{9,10},{10,11},{11... | collective-permute-start | bytes 98312 | tf_op jit(solution)/shard_map/ppermute | solution.py:20
  292.2 5.9 %collective-permute-start.14 = (f32[1,64,128]{2,1,0:T(8,128)S(1)}, f32[1,64,128]{2,1,0:T(8,128)S(1)}, u32[]{:S(2)}, u32[]{:S(2)}) collective-permute-start(f32[1,64,128]{2,1,0:T(8,128)S(1)} %get-tuple-element.9), channel_id=1, source_target_pairs={{1,0},{2,1},{3,2},{4,3},{5,4},{6,5},{7,6},{9,8},{10,9},{11,10},{12... | collective-permute-start | bytes 98312 | tf_op jit(solution)/shard_map/ppermute | solution.py:22
  295.8 6.7 %collective-permute-start.15 = (f32[1,64,128]{2,1,0:T(8,128)S(1)}, f32[1,64,128]{2,1,0:T(8,128)S(1)}, u32[]{:S(2)}, u32[]{:S(2)}) collective-permute-start(f32[1,64,128]{2,1,0:T(8,128)S(1)} %get-tuple-element.10), channel_id=1, source_target_pairs={{0,1},{1,2},{2,3},{3,4},{4,5},{5,6},{6,7},{8,9},{9,10},{10,11},{11... | collective-permute-start | bytes 98312 | tf_op jit(solution)/shard_map/ppermute | solution.py:20
  302.7 6.3 %collective-permute-start.16 = (f32[4,64,128]{2,1,0:T(8,128)S(1)}, f32[4,64,128]{2,1,0:T(8,128)S(1)}, u32[]{:S(2)}, u32[]{:S(2)}) collective-permute-start(f32[4,64,128]{2,1,0:T(8,128)S(1)} %fusion.135), channel_id=1, source_target_pairs={{0,8},{8,16},{16,24},{1,9},{9,17},{17,25},{2,10},{10,18},{18,26},{... | collective-permute-start | bytes 393224 | tf_op jit(solution)/shard_map/ppermute | solution.py:32
where the time goes:
time: 311 us; the launch traced here: 310 us
  local copies, waits for them, and re-layouts  109 us (35%)
  blocking collectives  86.2 us (28%)
  starting transfers between devices  50.4 us (16%)
  other arithmetic  35.4 us (11%)
  waiting for transfers between devices  27.6 us (9%)
    all_gather x2, blocking collectives, round_division(): lax.all_gather(lower_side, 'space', axis=0, tiled=True)  58.1 us
    reshape x7, local copies, waits for them, and re-layouts, mean_to_rougher(): field.reshape(extent_layout[0] // 2, 2, extent_layout[1] // 2, 2, extent_...  51.2 us
    reshape x6, local copies, waits for them, and re-layouts, lift_to_finer(): grown.reshape(2 * extent_layout[0], 2 * extent_layout[1], 2 * extent_layo...  31.1 us
    all_gather x1, blocking collectives, shards(): lax.all_gather(mid_cap, 'space', axis=0, tiled=True)  28.2 us
    ppermute x8, starting transfers between devices, with_halo(): lax.ppermute(head, axis, [((i + 1) % count, i) for i in range(ends)])  26.8 us
    reduce_sum x9, other arithmetic, mean_to_rougher(): return blocks.mean(axis=(1, 3, 5))  24.7 us
    ppermute x8, waiting for transfers between devices, with_halo(): lax.ppermute(tail, axis, [(i, (i + 1) % count) for i in range(ends)])  23.3 us
    ppermute x8, starting transfers between devices, with_halo(): lax.ppermute(tail, axis, [(i, (i + 1) % count) for i in range(ends)])  21.7 us
  transfers between devices with their start and end apart: 17, of which 7 were waited for; matrix products, arithmetic and copies ran while one was open for 9% of the time, Pallas kernels for 0%

commit v1 on v0

v1 whole, which is shorter than its diff:
```python
import functools

import jax
import jax.numpy as jnp
from jax import lax
from jax.experimental import pallas as pl
from jax.experimental.pallas import tpu as pltpu
from jax.sharding import PartitionSpec as P

COARSE_SWEEPS = 24
W = 0.8
F32 = jnp.float32
MESH = pl.DeviceIdType.MESH


def iota(shape, dim):
    return lax.broadcasted_iota(jnp.int32, shape, dim)


def dot(a, b):
    return jnp.dot(a, b, precision=lax.Precision.HIGHEST, preferred_element_type=F32)


def picks(lanes, pick, scale):
    src, dst = iota((lanes, lanes), 0), iota((lanes, lanes), 1)
    return jnp.where(pick(src, dst), scale, 0.0).astype(F32)


def in_plane(x, width):
    rows, lanes = x.shape[1], x.shape[2]
    lane, row = iota(x.shape, 2), iota(x.shape, 1)
    left, right = pltpu.roll(x, 1, 2), pltpu.roll(x, lanes - 1, 2)
    if width > lanes // 4:
        left = jnp.where(lane % width == 0, 0.0, left)
        right = jnp.where(lane % width == width - 1, 0.0, right)
    up = jnp.where(row == 0, 0.0, pltpu.roll(x, 1, 1))
    down = jnp.where(row == rows - 1, 0.0, pltpu.roll(x, rows - 1, 1))
    return (left + right) + (up + down)


def shifted(x):
    zero = jnp.zeros((1,) + x.shape[1:], F32)
    return jnp.concatenate([zero, x[:-1]], 0), jnp.concatenate([x[1:], zero], 0)


def sum_planes(x, width):
    before, after = shifted(x)
    return in_plane(x, width) + (before + after)


def sum_packed(x, width):
    half = pltpu.roll(x, width, 2)
    before, after = shifted(half)
    return in_plane(x, width) + (half + jnp.where(iota(x.shape, 2) < width, before, after))


def sum_inner(x, width):
    return in_plane(x[1:-1], width) + (x[:-2] + x[2:])


def flat(x):
    return x.reshape(x.shape[0] * x.shape[1], x.shape[2])


def kernel(
    parts, spans, steps,
    open_ref, src_ref, cap_in,
    fp_ref, up_ref,
    u0, src, cap, cx, gcap, gr, own, x1p, tmp, fin,
    in_sem, hs, hr, ks, kr, gs, gv, ts,
):
    me, span = lax.axis_index("space"), lax.axis_index("tm")
    depth, rows, lanes = open_ref.shape
    half = lanes // 2

    barrier = pltpu.get_barrier_semaphore()
    for k in range(1, parts):
        pl.semaphore_signal(barrier, inc=1, device_id={"space": (me + k) % parts}, device_id_type=MESH)
    for k in (1, spans - 1):
        pl.semaphore_signal(barrier, inc=1, device_id={"tm": (span + k) % spans}, device_id_type=MESH)

    loads = [
        pltpu.make_async_copy(cap_in, cap.at[pl.ds(2, depth)], in_sem.at[0]),
        pltpu.make_async_copy(open_ref, u0, in_sem.at[1]),
        pltpu.make_async_copy(src_ref, src, in_sem.at[2]),
    ]
    for load in loads:
        load.start()

    down_lo = picks(lanes, lambda s, d: (s // 2 == d) & (d < half), 0.125)
    down_hi = picks(lanes, lambda s, d: s // 2 + half == d, 0.125)
    down_2 = picks(lanes, lambda s, d: (s % half) // 2 == d, 0.125)
    down_3 = picks(lanes, lambda s, d: (s // 2 == d) & (s < half // 2), 0.125)
    up_lo = picks(lanes, lambda s, d: d // 2 == s, 1.0)
    up_hi = picks(lanes, lambda s, d: d // 2 + half == s, 1.0)
    up_2 = picks(lanes, lambda s, d: (d % half) // 2 == s, 1.0)
    up_3 = picks(lanes, lambda s, d: (d // 2 == s) & (d < half // 2), 1.0)

    def pair_rows(x):
        n, r, w = x.shape
        tmp[pl.ds(0, n * r), :] = flat(x)
        return tmp[pl.ds(0, n * r // 2, 2), :] + tmp[pl.ds(1, n * r // 2, 2), :]

    def twice_rows(x, planes):
        r = x.shape[0]
        tmp[pl.ds(0, r, 2), :] = x
        tmp[pl.ds(1, r, 2), :] = x
        return tmp[pl.ds(0, 2 * r), :].reshape(planes, 2 * r // planes, lanes)

    def pack(x):
        s = pair_rows(x.reshape(depth // 2, 2, rows, lanes).sum(1))
        n = rows // 2
        return dot(s[:n], down_lo) + dot(s[n:], down_hi)

    def to_2(x):
        return dot(pair_rows(x), down_2).reshape(parts, rows // 4, lanes)

    def to_3(x):
        s = x.reshape(parts // 2, 2, rows // 4, lanes).sum(1)
        return dot(pair_rows(s), down_3).reshape(parts // 2, rows // 8, lanes)

    def halo(buf, sends, recvs, at, up, down):
        to_next = pltpu.make_async_remote_copy(
            buf.at[pl.ds(*up[0])], buf.at[pl.ds(*up[1])], sends.at[at], recvs.at[at],
            device_id={"space": (me + 1) % parts}, device_id_type=MESH)
        to_prev = pltpu.make_async_remote_copy(
            buf.at[pl.ds(*down[0])], buf.at[pl.ds(*down[1])], sends.at[at + 1], recvs.at[at + 1],
            device_id={"space": (me + parts - 1) % parts}, device_id_type=MESH)
        return to_next, to_prev

    def begin(pair):
        @pl.when(me < parts - 1)
        def _():
            pair[0].start()

        @pl.when(me > 0)
        def _():
            pair[1].start()

    def arrive(pair):
        @pl.when(me > 0)
        def _():
            pair[0].wait_recv()

        @pl.when(me < parts - 1)
        def _():
            pair[1].wait_recv()

    def sent(pair):
        @pl.when(me < parts - 1)
        def _():
            pair[0].wait_send()

        @pl.when(me > 0)
        def _():
            pair[1].wait_send()

    def gather(buf, sends, recvs, row):
        return [
            pltpu.make_async_remote_copy(
                buf.at[me], buf.at[me], sends.at[row, k], recvs.at[row, k],
                device_id={"space": (me + k) % parts}, device_id_type=MESH)
            for k in range(1, parts)
        ]

    near = [halo(cx.at[t], hs, hr, 4 * t, ((depth + 1, 2), (1, 2)), ((3, 2), (depth + 3, 2))) for t in range(steps)]
    far = [halo(cx.at[t], hs, hr, 4 * t + 2, ((depth, 1), (0, 1)), ((5, 1), (depth + 5, 1))) for t in range(steps)]
    caps = halo(cap, ks, kr, 0, ((depth, 2), (0, 2)), ((2, 2), (depth + 2, 2)))
    gather_cap = gather(gcap, gs, gv, 0)
    gather_r = [gather(gr.at[t], gs, gv, 1 + t) for t in range(steps)]

    @pl.when(me == 0)
    def _():
        cap[0:2] = jnp.zeros((2, rows, lanes), F32)
        for t in range(steps):
            cx[t, 0:3] = jnp.zeros((3, rows, lanes), F32)

    @pl.when(me == parts - 1)
    def _():
        cap[depth + 2:] = jnp.zeros((2, rows, lanes), F32)
        for t in range(steps):
            cx[t, depth + 3:] = jnp.zeros((3, rows, lanes), F32)

    x1p[0] = jnp.zeros(x1p.shape[1:], F32)
    x1p[parts + 1] = jnp.zeros(x1p.shape[1:], F32)

    loads[0].wait()
    mine = cap[2:2 + depth]
    gcap[me] = pack(mine)
    loads[1].wait()
    loads[2].wait()
    b = mine * u0[...] + src[0]
    own[...] = b
    cx[0, 3:3 + depth] = b * (W / (mine + 6.0))

    pl.semaphore_wait(barrier, parts - 1 + 2)
    begin(near[0])
    begin(caps)
    for copy in gather_cap:
        copy.start()
    begin(far[0])

    arrive(caps)
    plane = me * depth - 2 + iota((depth + 4, 1, 1), 0)
    inside = (plane >= 0) & (plane < parts * depth)
    a0 = jnp.where(inside, W / (cap[...] + 6.0), 0.0)
    cells = None

    for t in range(steps):
        last = t == steps - 1
        arrive(near[t])
        c = cx[t, 1:depth + 5]
        x = 1.2 * c[1:-1] + a0[1:-1] * sum_inner(c, lanes)
        inner = x[1:-1]
        d0 = cap[2:2 + depth] + 6.0
        r = own[...] - d0 * inner + sum_inner(x, lanes)
        gr[t, me] = pack(r)
        for copy in gather_r[t]:
            copy.start()

        arrive(far[t])
        first = 1.2 * cx[t, 1:2] + a0[0:1] * sum_inner(cx[t, 0:3], lanes)
        final = 1.2 * cx[t, depth + 4:depth + 5] + a0[-1:] * sum_inner(cx[t, depth + 3:depth + 6], lanes)
        x = jnp.concatenate([first, x, final], 0)

        if t == 0:
            for copy in gather_cap:
                copy.wait_recv()
            cap1 = gcap[...]
            i1 = W / (cap1 + 3.0)
            cap2 = to_2(cap1)
            i2 = jnp.where(iota(cap2.shape, 2) < lanes // 4, W / (cap2 + 1.5), 0.0)
            cap3 = to_3(cap2)
            i3 = jnp.where(iota(cap3.shape, 2) < lanes // 8, W / (cap3 + 0.75), 0.0)
            a1, a2, a3 = 0.5 * i1, 0.25 * i2, 0.125 * i3

        for copy in gather_r[t]:
            copy.wait_recv()
        b1 = gr[t]
        c1 = b1 * i1
        y1 = 1.2 * c1 + a1 * sum_packed(c1, half)
        r1 = b1 - (cap1 + 3.0) * y1 + 0.5 * sum_packed(y1, half)
        b2 = to_2(r1)
        c2 = b2 * i2
        y2 = 1.2 * c2 + a2 * sum_planes(c2, lanes // 4)
        r2 = b2 - (cap2 + 1.5) * y2 + 0.25 * sum_planes(y2, lanes // 4)
        c3 = to_3(r2) * i3
        y3 = lax.fori_loop(
            0, COARSE_SWEEPS - 1,
            lambda _, y: (0.2 * y + c3) + a3 * sum_planes(y, lanes // 8), c3, unroll=True)
        lift = twice_rows(dot(flat(y3), up_3), parts // 2)
        lift = jnp.broadcast_to(lift[:, None], (parts // 2, 2) + lift.shape[1:]).reshape(y2.shape)
        y2 = y2 + lift
        for _ in range(2):
            y2 = (0.2 * y2 + c2) + a2 * sum_planes(y2, lanes // 4)
        y1 = y1 + twice_rows(dot(flat(y2), up_2), parts)
        for _ in range(2):
            y1 = (0.2 * y1 + c1) + a1 * sum_packed(y1, half)
        x1p[1:parts + 1] = y1

        odd = dot(flat(x1p[pl.ds(me, 2)]), up_hi)
        even = dot(flat(x1p[pl.ds(me + 1, 2)]), up_lo)
        n = rows // 2
        lift = twice_rows(jnp.concatenate([odd[:n], even[:n], odd[n:], even[n:]], 0), depth // 2 + 2)
        lift = jnp.broadcast_to(lift[:, None], (depth // 2 + 2, 2) + lift.shape[1:]).reshape(x.shape)
        x = x + lift
        x = (0.2 * x[1:-1] + cx[t, 2:depth + 4]) + a0[1:-1] * sum_inner(x, lanes)
        x = (0.2 * x[1:-1] + cx[t, 3:depth + 3]) + a0[2:-2] * sum_inner(x, lanes)
        if t == 0:
            fp_ref[...] = x
        if not last:
            b = cap[2:2 + depth] * x + src[t + 1]
            own[...] = b
            cx[t + 1, 3:3 + depth] = b * a0[2:-2]
            begin(near[t + 1])
            begin(far[t + 1])
        else:
            fin[...] = x

    onward = pltpu.make_async_remote_copy(
        fin, up_ref, ts.at[0], ts.at[1],
        device_id={"tm": (span + 1) % spans}, device_id_type=MESH)

    @pl.when(span < spans - 1)
    def _():
        onward.start()

    @pl.when(span == 0)
    def _():
        up_ref[...] = u0[...]

    for pair in near + far + [caps]:
        sent(pair)
    for copies in [gather_cap] + gather_r:
        for copy in copies:
            copy.wait_send()

    @pl.when(span < spans - 1)
    def _():
        onward.wait_send()

    @pl.when(span > 0)
    def _():
        onward.wait_recv()


def shards(span_opening, source_power, warmth_retention):
    parts, spans = lax.axis_size("space"), lax.axis_size("tm")
    steps = source_power.shape[1]
    depth, rows, lanes = warmth_retention.shape
    slab = jax.ShapeDtypeStruct((depth, rows, lanes), F32)
    vmem = pl.BlockSpec(memory_space=pltpu.VMEM)
    dma = pltpu.SemaphoreType.DMA
    fpoint, updated = pl.pallas_call(
        functools.partial(kernel, parts, spans, steps),
        out_shape=(slab, slab),
        in_specs=[pl.BlockSpec(memory_space=pl.ANY)] * 3,
        out_specs=(vmem, vmem),
        scratch_shapes=[
            pltpu.VMEM((depth, rows, lanes), F32),
            pltpu.VMEM((steps, depth, rows, lanes), F32),
            pltpu.VMEM((depth + 4, rows, lanes), F32),
            pltpu.VMEM((steps, depth + 6, rows, lanes), F32),
            pltpu.VMEM((parts, rows // 2, lanes), F32),
            pltpu.VMEM((steps, parts, rows // 2, lanes), F32),
            pltpu.VMEM((depth, rows, lanes), F32),
            pltpu.VMEM((parts + 2, rows // 2, lanes), F32),
            pltpu.VMEM((max(parts * rows // 2, (depth // 2 + 2) * rows), lanes), F32),
            pltpu.VMEM((depth, rows, lanes), F32),
            dma((3,)), dma((4 * steps,)), dma((4 * steps,)), dma((2,)), dma((2,)),
            dma((1 + steps, parts)), dma((1 + steps, parts)), dma((2,)),
        ],
        compiler_params=pltpu.CompilerParams(
            collective_id=0, has_side_effects=True, vmem_limit_bytes=48 * 1024 * 1024
        ),
    )(span_opening[0], source_power[0], warmth_retention)
    return fpoint[None], updated[None]


def solution(mesh):
    in_specs = (
        P("tm", "space", None, None),
        P("tm", None, "space", None, None),
        P("space", None, None),
    )
    out_specs = (P("tm", "space", None, None), P("tm", "space", None, None))
    return jax.shard_map(shards, mesh=mesh, in_specs=in_specs, out_specs=out_specs, check_vma=False)
```

time: 311 us -> 43.4 us (0.14)
  the two profiles are of different devices: /device:TPU:10 before, /device:TPU:0 now
where the time goes in v1:
time: 43.4 us; the launch traced here: 43.2 us
  Pallas kernels  38.5 us (89%)
  local copies, waits for them, and re-layouts  4.06 us (9%)
  between operations  0.65 us (1%)
    pallas_call x1, Pallas kernels, shards(): pl.pallas_call(functools.partial(kernel, parts, spans, steps), out_shape=...  38.5 us
    unnamed x8, local copies, waits for them, and re-layouts  4.06 us

profile of v1, /device:TPU:0, one launch (start us, length us, event | category | flops | bytes accessed | tf_op | source)
XLA Modules:
  0.0 43.2 jit_solution(11833489763976394290)
XLA Ops:
  0.6 0.0 copy-start
  0.6 0.9 %copy-done = f32[1,2,4,64,128]{4,3,2,1,0:T(8,128)S(1)} copy-done((f32[1,2,4,64,128]{4,3,2,1,0:T(8,128)S(1)}, f32[1,2,4,64,128]{4,3,2,1,0:T(8,128)}, u32[]{:S(2)}) %copy-start) | copy-done | bytes 262168
  1.6 0.0 copy-start.1
  1.6 0.9 %copy-done.1 = f32[1,4,64,128]{3,2,1,0:T(8,128)S(1)} copy-done((f32[1,4,64,128]{3,2,1,0:T(8,128)S(1)}, f32[1,4,64,128]{3,2,1,0:T(8,128)}, u32[]{:S(2)}) %copy-start.1) | copy-done | bytes 131096
  2.5 0.0 copy-start.2
  2.5 0.9 %copy-done.2 = f32[4,64,128]{2,1,0:T(8,128)S(1)} copy-done((f32[4,64,128]{2,1,0:T(8,128)S(1)}, f32[4,64,128]{2,1,0:T(8,128)}, u32[]{:S(2)}) %copy-start.2) | copy-done | bytes 131096
  3.4 38.5 %shard_map.50 = (f32[4,64,128]{2,1,0:T(8,128)S(1)}, f32[4,64,128]{2,1,0:T(8,128)S(1)}) custom-call(f32[4,64,128]{2,1,0:T(8,128)S(1)} %bitcast.7, f32[2,4,64,128]{3,2,1,0:T(8,128)S(1)} %bitcast.4, f32[4,64,128]{2,1,0:T(8,128)S(1)} %copy-done.2), custom_call_target="tpu_custom_call" | custom-call | tf_op jit(solution)/shard_map/pallas_call | solution.py:314
  41.9 0.7 %copy.7 = f32[1,4,64,128]{3,2,1,0:T(8,128)} copy(f32[1,4,64,128]{3,2,1,0:T(8,128)S(1)} %bitcast.6) | data formatting | bytes 262144
  42.6 0.7 %copy.8 = f32[1,4,64,128]{3,2,1,0:T(8,128)} copy(f32[1,4,64,128]{3,2,1,0:T(8,128)S(1)} %bitcast.5) | data formatting | bytes 262144
Async XLA Ops:
  0.6 1.0 %copy-start = (f32[1,2,4,64,128]{4,3,2,1,0:T(8,128)S(1)}, f32[1,2,4,64,128]{4,3,2,1,0:T(8,128)}, u32[]{:S(2)}) copy-start(f32[1,2,4,64,128]{4,3,2,1,0:T(8,128)} %param.4) | copy-start | bytes 786436
  1.6 0.9 %copy-start.1 = (f32[1,4,64,128]{3,2,1,0:T(8,128)S(1)}, f32[1,4,64,128]{3,2,1,0:T(8,128)}, u32[]{:S(2)}) copy-start(f32[1,4,64,128]{3,2,1,0:T(8,128)} %param.3) | copy-start | bytes 393220
  2.5 0.9 %copy-start.2 = (f32[4,64,128]{2,1,0:T(8,128)S(1)}, f32[4,64,128]{2,1,0:T(8,128)}, u32[]{:S(2)}) copy-start(f32[4,64,128]{2,1,0:T(8,128)} %cap_in.1) | copy-start | bytes 393220

commit v2 on v1

--- a/solution.py
+++ b/solution.py
@@ -165,7 +165,8 @@
 
     near = [halo(cx.at[t], hs, hr, 4 * t, ((depth + 1, 2), (1, 2)), ((3, 2), (depth + 3, 2))) for t in range(steps)]
     far = [halo(cx.at[t], hs, hr, 4 * t + 2, ((depth, 1), (0, 1)), ((5, 1), (depth + 5, 1))) for t in range(steps)]
-    caps = halo(cap, ks, kr, 0, ((depth, 2), (0, 2)), ((2, 2), (depth + 2, 2)))
+    cap_near = halo(cap, ks, kr, 0, ((depth + 1, 1), (1, 1)), ((2, 1), (depth + 2, 1)))
+    cap_far = halo(cap, ks, kr, 2, ((depth, 1), (0, 1)), ((3, 1), (depth + 3, 1)))
     gather_cap = gather(gcap, gs, gv, 0)
     gather_r = [gather(gr.at[t], gs, gv, 1 + t) for t in range(steps)]
 
@@ -194,36 +195,33 @@
     cx[0, 3:3 + depth] = b * (W / (mine + 6.0))
 
     pl.semaphore_wait(barrier, parts - 1 + 2)
+    begin(cap_near)
     begin(near[0])
-    begin(caps)
     for copy in gather_cap:
         copy.start()
-    begin(far[0])
-
-    arrive(caps)
-    plane = me * depth - 2 + iota((depth + 4, 1, 1), 0)
-    inside = (plane >= 0) & (plane < parts * depth)
-    a0 = jnp.where(inside, W / (cap[...] + 6.0), 0.0)
-    cells = None
+
+    def weights(start, count):
+        plane = me * depth - 2 + start + iota((count, 1, 1), 0)
+        inside = (plane >= 0) & (plane < parts * depth)
+        return jnp.where(inside, W / (cap[start:start + count] + 6.0), 0.0)
+
+    arrive(cap_near)
+    a = weights(1, depth + 2)
 
     for t in range(steps):
         last = t == steps - 1
         arrive(near[t])
         c = cx[t, 1:depth + 5]
-        x = 1.2 * c[1:-1] + a0[1:-1] * sum_inner(c, lanes)
+        x = 1.2 * c[1:-1] + a * sum_inner(c, lanes)
         inner = x[1:-1]
         d0 = cap[2:2 + depth] + 6.0
         r = own[...] - d0 * inner + sum_inner(x, lanes)
         gr[t, me] = pack(r)
         for copy in gather_r[t]:
             copy.start()
-
-        arrive(far[t])
-        first = 1.2 * cx[t, 1:2] + a0[0:1] * sum_inner(cx[t, 0:3], lanes)
-        final = 1.2 * cx[t, depth + 4:depth + 5] + a0[-1:] * sum_inner(cx[t, depth + 3:depth + 6], lanes)
-        x = jnp.concatenate([first, x, final], 0)
-
+        begin(far[t])
         if t == 0:
+            begin(cap_far)
             for copy in gather_cap:
                 copy.wait_recv()
             cap1 = gcap[...]
@@ -262,18 +260,23 @@
         even = dot(flat(x1p[pl.ds(me + 1, 2)]), up_lo)
         n = rows // 2
         lift = twice_rows(jnp.concatenate([odd[:n], even[:n], odd[n:], even[n:]], 0), depth // 2 + 2)
-        lift = jnp.broadcast_to(lift[:, None], (depth // 2 + 2, 2) + lift.shape[1:]).reshape(x.shape)
-        x = x + lift
-        x = (0.2 * x[1:-1] + cx[t, 2:depth + 4]) + a0[1:-1] * sum_inner(x, lanes)
-        x = (0.2 * x[1:-1] + cx[t, 3:depth + 3]) + a0[2:-2] * sum_inner(x, lanes)
+        lift = jnp.broadcast_to(lift[:, None], (depth // 2 + 2, 2) + lift.shape[1:]).reshape(depth + 4, rows, lanes)
+        arrive(far[t])
+        if t == 0:
+            arrive(cap_far)
+            a_lo, a_hi = weights(0, 1), weights(depth + 3, 1)
+        first = 1.2 * cx[t, 1:2] + a_lo * sum_inner(cx[t, 0:3], lanes)
+        final = 1.2 * cx[t, depth + 4:depth + 5] + a_hi * sum_inner(cx[t, depth + 3:depth + 6], lanes)
+        x = jnp.concatenate([first, x, final], 0) + lift
+        x = (0.2 * x[1:-1] + cx[t, 2:depth + 4]) + a * sum_inner(x, lanes)
+        x = (0.2 * x[1:-1] + cx[t, 3:depth + 3]) + a[1:-1] * sum_inner(x, lanes)
         if t == 0:
             fp_ref[...] = x
         if not last:
             b = cap[2:2 + depth] * x + src[t + 1]
             own[...] = b
-            cx[t + 1, 3:3 + depth] = b * a0[2:-2]
+            cx[t + 1, 3:3 + depth] = b * a[1:-1]
             begin(near[t + 1])
-            begin(far[t + 1])
         else:
             fin[...] = x
 
@@ -289,7 +292,7 @@
     def _():
         up_ref[...] = u0[...]
 
-    for pair in near + far + [caps]:
+    for pair in near + far + [cap_near, cap_far]:
         sent(pair)
     for copies in [gather_cap] + gather_r:
         for copy in copies:
@@ -313,7 +316,7 @@
     dma = pltpu.SemaphoreType.DMA
     fpoint, updated = pl.pallas_call(
         functools.partial(kernel, parts, spans, steps),
-        out_shape=(slab, slab),
+        out_shape=(pltpu.VMEM(slab.shape, F32),) * 2,
         in_specs=[pl.BlockSpec(memory_space=pl.ANY)] * 3,
         out_specs=(vmem, vmem),
         scratch_shapes=[
@@ -327,11 +330,11 @@
             pltpu.VMEM((parts + 2, rows // 2, lanes), F32),
             pltpu.VMEM((max(parts * rows // 2, (depth // 2 + 2) * rows), lanes), F32),
             pltpu.VMEM((depth, rows, lanes), F32),
-            dma((3,)), dma((4 * steps,)), dma((4 * steps,)), dma((2,)), dma((2,)),
+            dma((3,)), dma((4 * steps,)), dma((4 * steps,)), dma((4,)), dma((4,)),
             dma((1 + steps, parts)), dma((1 + steps, parts)), dma((2,)),
         ],
         compiler_params=pltpu.CompilerParams(
-            collective_id=0, has_side_effects=True, vmem_limit_bytes=48 * 1024 * 1024
+            collective_id=0, has_side_effects=True, vmem_limit_bytes=67043328 - 2 * 4 * slab.size
         ),
     )(span_opening[0], source_power[0], warmth_retention)
     return fpoint[None], updated[None]

time: 43.4 us -> 39.3 us (0.906)
  local copies, waits for them, and re-layouts: 4.06 us -> 1.31 us
  Pallas kernels: 38.5 us -> 37.2 us
    unnamed x8 -> x2, local copies, waits for them, and re-layouts: 4.06 us -> 1.31 us
    pallas_call x1, Pallas kernels: 38.5 us -> 37.2 us  [shards(): pl.pallas_call(functools.partial(kernel, parts, spans, steps), out_shape=...]
where the time goes in v2:
time: 39.3 us; the launch traced here: 39.2 us
  Pallas kernels  37.2 us (95%)
  local copies, waits for them, and re-layouts  1.31 us (3%)
  between operations  0.64 us (2%)
    pallas_call x1, Pallas kernels, shards(): pl.pallas_call(functools.partial(kernel, parts, spans, steps), out_shape=...  37.2 us
    unnamed x2, local copies, waits for them, and re-layouts  1.31 us

profile of v2, /device:TPU:0, one launch (start us, length us, event | category | flops | bytes accessed | tf_op | source)
XLA Modules:
  0.0 39.2 jit_solution(788189635775626336)
XLA Ops:
  0.6 37.2 %shard_map.50 = (f32[4,64,128]{2,1,0:T(8,128)S(1)}, f32[4,64,128]{2,1,0:T(8,128)S(1)}) custom-call(f32[4,64,128]{2,1,0:T(8,128)} %bitcast.7, f32[2,4,64,128]{3,2,1,0:T(8,128)} %bitcast.6, f32[4,64,128]{2,1,0:T(8,128)} %cap_in.1), custom_call_target="tpu_custom_call" | custom-call | tf_op jit(solution)/shard_map/pallas_call | solution.py:317
  37.9 0.7 %copy.7 = f32[1,4,64,128]{3,2,1,0:T(8,128)} copy(f32[1,4,64,128]{3,2,1,0:T(8,128)S(1)} %bitcast.5) | data formatting | bytes 262144
  38.5 0.7 %copy.8 = f32[1,4,64,128]{3,2,1,0:T(8,128)} copy(f32[1,4,64,128]{3,2,1,0:T(8,128)S(1)} %bitcast.4) | data formatting | bytes 262144

commit v3 on v2

--- a/solution.py
+++ b/solution.py
@@ -66,8 +66,8 @@
     parts, spans, steps,
     open_ref, src_ref, cap_in,
     fp_ref, up_ref,
-    u0, src, cap, cx, gcap, gr, own, x1p, tmp, fin,
-    in_sem, hs, hr, ks, kr, gs, gv, ts,
+    u0, src0, src1, cap, c0, c1x, gcap, gr, own, x1p, tmp, fin,
+    in_sem, hs, hr, ks, kr, fs, fr, gs, gv, ts,
 ):
     me, span = lax.axis_index("space"), lax.axis_index("tm")
     depth, rows, lanes = open_ref.shape
@@ -76,13 +76,14 @@
     barrier = pltpu.get_barrier_semaphore()
     for k in range(1, parts):
         pl.semaphore_signal(barrier, inc=1, device_id={"space": (me + k) % parts}, device_id_type=MESH)
-    for k in (1, spans - 1):
+    for k in range(1, spans):
         pl.semaphore_signal(barrier, inc=1, device_id={"tm": (span + k) % spans}, device_id_type=MESH)
 
     loads = [
-        pltpu.make_async_copy(cap_in, cap.at[pl.ds(2, depth)], in_sem.at[0]),
+        pltpu.make_async_copy(cap_in, cap.at[pl.ds(depth, depth)], in_sem.at[0]),
         pltpu.make_async_copy(open_ref, u0, in_sem.at[1]),
-        pltpu.make_async_copy(src_ref, src, in_sem.at[2]),
+        pltpu.make_async_copy(src_ref.at[0], src0, in_sem.at[2]),
+        pltpu.make_async_copy(src_ref.at[1], src1.at[pl.ds(2, depth)], in_sem.at[3]),
     ]
     for load in loads:
         load.start()
@@ -119,41 +120,71 @@
         s = x.reshape(parts // 2, 2, rows // 4, lanes).sum(1)
         return dot(pair_rows(s), down_3).reshape(parts // 2, rows // 8, lanes)
 
-    def halo(buf, sends, recvs, at, up, down):
-        to_next = pltpu.make_async_remote_copy(
-            buf.at[pl.ds(*up[0])], buf.at[pl.ds(*up[1])], sends.at[at], recvs.at[at],
-            device_id={"space": (me + 1) % parts}, device_id_type=MESH)
-        to_prev = pltpu.make_async_remote_copy(
-            buf.at[pl.ds(*down[0])], buf.at[pl.ds(*down[1])], sends.at[at + 1], recvs.at[at + 1],
-            device_id={"space": (me + parts - 1) % parts}, device_id_type=MESH)
-        return to_next, to_prev
+    def halo(buf, sends, recvs, at, count, up, down, reach=1, rows_at=None):
+        def cut(start):
+            return buf.at[pl.ds(start, count)] if rows_at is None else buf.at[pl.ds(start, count), rows_at]
+
+        ways = ((up, reach, at), (down, parts - reach, at + 1))
+        pair = [
+            pltpu.make_async_remote_copy(
+                cut(way[0]), cut(way[1]), sends.at[sem], recvs.at[sem],
+                device_id={"space": (me + by) % parts}, device_id_type=MESH)
+            for way, by, sem in ways
+        ]
+        return pair + [reach]
 
     def begin(pair):
+        @pl.when(me < parts - pair[2])
+        def _():
+            pair[0].start()
+
+        @pl.when(me >= pair[2])
+        def _():
+            pair[1].start()
+
+    def arrive(pair):
+        @pl.when(me >= pair[2])
+        def _():
+            pair[0].wait_recv()
+
+        @pl.when(me < parts - pair[2])
+        def _():
+            pair[1].wait_recv()
+
+    def sent(pair):
+        @pl.when(me < parts - pair[2])
+        def _():
+            pair[0].wait_send()
+
+        @pl.when(me >= pair[2])
+        def _():
+            pair[1].wait_send()
+
+    share = rows // spans
+    my_rows = pl.ds(pl.multiple_of(span * share, share), share)
+
+    def hand_on(at, count, below, above):
+        def copies(start, sem):
+            return [
+                pltpu.make_async_remote_copy(
+                    cap.at[pl.ds(start, count), my_rows], cap.at[pl.ds(start, count), my_rows],
+                    fs.at[sem, k], fr.at[sem, k],
+                    device_id={"tm": (span + k) % spans}, device_id_type=MESH)
+                for k in range(1, spans)
+            ]
+
+        return copies(below, at), copies(above, at + 1)
+
+    def each(pair, act):
+        @pl.when(me > 0)
+        def _():
+            for copy in pair[0]:
+                act(copy)
+
         @pl.when(me < parts - 1)
         def _():
-            pair[0].start()
-
-        @pl.when(me > 0)
-        def _():
-            pair[1].start()
-
-    def arrive(pair):
-        @pl.when(me > 0)
-        def _():
-            pair[0].wait_recv()
-
-        @pl.when(me < parts - 1)
-        def _():
-            pair[1].wait_recv()
-
-    def sent(pair):
-        @pl.when(me < parts - 1)
-        def _():
-            pair[0].wait_send()
-
-        @pl.when(me > 0)
-        def _():
-            pair[1].wait_send()
+            for copy in pair[1]:
+                act(copy)
 
     def gather(buf, sends, recvs, row):
         return [
@@ -163,65 +194,93 @@
             for k in range(1, parts)
         ]
 
-    near = [halo(cx.at[t], hs, hr, 4 * t, ((depth + 1, 2), (1, 2)), ((3, 2), (depth + 3, 2))) for t in range(steps)]
-    far = [halo(cx.at[t], hs, hr, 4 * t + 2, ((depth, 1), (0, 1)), ((5, 1), (depth + 5, 1))) for t in range(steps)]
-    cap_near = halo(cap, ks, kr, 0, ((depth + 1, 1), (1, 1)), ((2, 1), (depth + 2, 1)))
-    cap_far = halo(cap, ks, kr, 2, ((depth, 1), (0, 1)), ((3, 1), (depth + 3, 1)))
+    d = depth
+    near = halo(c0, hs, hr, 0, 2, (2 * d - 1, d - 1), (d + 1, 2 * d + 1))
+    far = halo(c0, hs, hr, 2, d - 2, (d + 1, 1), (d + 3, 2 * d + 3))
+    beyond = halo(c0, hs, hr, 4, 1, (2 * d, 0), (d + 1, 3 * d + 1), reach=2)
+    source = halo(src1, hs, hr, 6, 2, (d, 0), (2, d + 2))
+    third = halo(c1x, hs, hr, 8, 1, (d, 0), (5, d + 5))
+    cap_near = halo(cap, ks, kr, 0, 1, (2 * d - 1, d - 1), (d, 2 * d), rows_at=my_rows)
+    cap_far = halo(cap, ks, kr, 2, d - 1, (d, 0), (d + 1, 2 * d + 1), rows_at=my_rows)
+    pass_near = hand_on(0, 1, d - 1, 2 * d)
+    pass_far = hand_on(2, d - 1, 0, 2 * d + 1)
     gather_cap = gather(gcap, gs, gv, 0)
     gather_r = [gather(gr.at[t], gs, gv, 1 + t) for t in range(steps)]
 
+    def clear(ref, start, stop):
+        ref[start:stop] = jnp.zeros((stop - start, rows, lanes), F32)
+
     @pl.when(me == 0)
     def _():
-        cap[0:2] = jnp.zeros((2, rows, lanes), F32)
-        for t in range(steps):
-            cx[t, 0:3] = jnp.zeros((3, rows, lanes), F32)
+        clear(cap, 0, d)
+        clear(c0, 0, d + 1)
+        clear(c1x, 0, 3)
+        clear(src1, 0, 2)
+
+    @pl.when(me == 1)
+    def _():
+        clear(c0, 0, 1)
+
+    @pl.when(me == parts - 2)
+    def _():
+        clear(c0, 3 * d + 1, 3 * d + 2)
 
     @pl.when(me == parts - 1)
     def _():
-        cap[depth + 2:] = jnp.zeros((2, rows, lanes), F32)
-        for t in range(steps):
-            cx[t, depth + 3:] = jnp.zeros((3, rows, lanes), F32)
+        clear(cap, 2 * d, 3 * d)
+        clear(c0, 2 * d + 1, 3 * d + 2)
+        clear(c1x, d + 3, d + 6)
+        clear(src1, d + 2, d + 4)
 
     x1p[0] = jnp.zeros(x1p.shape[1:], F32)
     x1p[parts + 1] = jnp.zeros(x1p.shape[1:], F32)
 
     loads[0].wait()
-    mine = cap[2:2 + depth]
+    mine = cap[d:2 * d]
     gcap[me] = pack(mine)
     loads[1].wait()
     loads[2].wait()
-    b = mine * u0[...] + src[0]
+    b = mine * u0[...] + src0[...]
     own[...] = b
-    cx[0, 3:3 + depth] = b * (W / (mine + 6.0))
-
-    pl.semaphore_wait(barrier, parts - 1 + 2)
+    c0[d + 1:2 * d + 1] = b * (W / (mine + 6.0))
+    loads[3].wait()
+
+    pl.semaphore_wait(barrier, parts - 1 + spans - 1)
     begin(cap_near)
-    begin(near[0])
+    begin(near)
     for copy in gather_cap:
         copy.start()
 
     def weights(start, count):
-        plane = me * depth - 2 + start + iota((count, 1, 1), 0)
+        plane = (me - 1) * depth + start + iota((count, 1, 1), 0)
         inside = (plane >= 0) & (plane < parts * depth)
         return jnp.where(inside, W / (cap[start:start + count] + 6.0), 0.0)
 
     arrive(cap_near)
-    a = weights(1, depth + 2)
+    each(pass_near, lambda copy: copy.start())
+    each(pass_near, lambda copy: copy.wait_recv())
+    a = weights(d - 1, d + 2)
 
     for t in range(steps):
-        last = t == steps - 1
-        arrive(near[t])
-        c = cx[t, 1:depth + 5]
+        if t == 0:
+            arrive(near)
+            c = c0[d - 1:2 * d + 3]
+        else:
+            c = c1x[1:d + 5]
         x = 1.2 * c[1:-1] + a * sum_inner(c, lanes)
         inner = x[1:-1]
-        d0 = cap[2:2 + depth] + 6.0
+        d0 = cap[d:2 * d] + 6.0
         r = own[...] - d0 * inner + sum_inner(x, lanes)
         gr[t, me] = pack(r)
         for copy in gather_r[t]:
             copy.start()
-        begin(far[t])
-        if t == 0:
+        if t == 1:
+            begin(third)
+        else:
             begin(cap_far)
+            begin(far)
+            begin(beyond)
+            begin(source)
             for copy in gather_cap:
                 copy.wait_recv()
             cap1 = gcap[...]
@@ -243,6 +302,9 @@
         y2 = 1.2 * c2 + a2 * sum_planes(c2, lanes // 4)
         r2 = b2 - (cap2 + 1.5) * y2 + 0.25 * sum_planes(y2, lanes // 4)
         c3 = to_3(r2) * i3
+        if t == 0:
+            arrive(cap_far)
+            each(pass_far, lambda copy: copy.start())
         y3 = lax.fori_loop(
             0, COARSE_SWEEPS - 1,
             lambda _, y: (0.2 * y + c3) + a3 * sum_planes(y, lanes // 8), c3, unroll=True)
@@ -256,29 +318,38 @@
             y1 = (0.2 * y1 + c1) + a1 * sum_packed(y1, half)
         x1p[1:parts + 1] = y1
 
-        odd = dot(flat(x1p[pl.ds(me, 2)]), up_hi)
-        even = dot(flat(x1p[pl.ds(me + 1, 2)]), up_lo)
         n = rows // 2
-        lift = twice_rows(jnp.concatenate([odd[:n], even[:n], odd[n:], even[n:]], 0), depth // 2 + 2)
-        lift = jnp.broadcast_to(lift[:, None], (depth // 2 + 2, 2) + lift.shape[1:]).reshape(depth + 4, rows, lanes)
-        arrive(far[t])
+        around = flat(x1p[pl.ds(me, 3)])
+        even, odd = dot(around, up_lo), dot(around, up_hi)
+        halves = [part[n * k:n * k + n] for k in range(3) for part in (even, odd)]
+        if t == 1:
+            halves = halves[1:-1]
+        planes = len(halves)
+        lift = twice_rows(jnp.concatenate(halves, 0), planes)
+        lift = jnp.broadcast_to(lift[:, None], (planes, 2) + lift.shape[1:]).reshape(2 * planes, rows, lanes)
         if t == 0:
-            arrive(cap_far)
-            a_lo, a_hi = weights(0, 1), weights(depth + 3, 1)
-        first = 1.2 * cx[t, 1:2] + a_lo * sum_inner(cx[t, 0:3], lanes)
-        final = 1.2 * cx[t, depth + 4:depth + 5] + a_hi * sum_inner(cx[t, depth + 3:depth + 6], lanes)
-        x = jnp.concatenate([first, x, final], 0) + lift
-        x = (0.2 * x[1:-1] + cx[t, 2:depth + 4]) + a * sum_inner(x, lanes)
-        x = (0.2 * x[1:-1] + cx[t, 3:depth + 3]) + a[1:-1] * sum_inner(x, lanes)
-        if t == 0:
-            fp_ref[...] = x
-        if not last:
-            b = cap[2:2 + depth] * x + src[t + 1]
-            own[...] = b
-            cx[t + 1, 3:3 + depth] = b * a[1:-1]
-            begin(near[t + 1])
+            each(pass_far, lambda copy: copy.wait_recv())
+            arrive(far)
+            arrive(beyond)
+            a_lo, a_hi = weights(0, d - 1), weights(2 * d + 1, d - 1)
+            first = 1.2 * c0[1:d] + a_lo * sum_inner(c0[0:d + 1], lanes)
+            final = 1.2 * c0[2 * d + 2:3 * d + 1] + a_hi * sum_inner(c0[2 * d + 1:3 * d + 2], lanes)
+            wide = jnp.concatenate([a_lo, a, a_hi], 0)
+            x = jnp.concatenate([first, x, final], 0) + lift
+            x = (0.2 * x[1:-1] + c0[2:3 * d]) + wide[1:-1] * sum_inner(x, lanes)
+            x = (0.2 * x[1:-1] + c0[3:3 * d - 1]) + wide[2:-2] * sum_inner(x, lanes)
+            fp_ref[...] = x[2:-2]
+            arrive(source)
+            b = cap[2:3 * d - 2] * x + src1[...]
+            own[...] = b[2:-2]
+            c1x[1:d + 5] = b * wide[2:-2]
         else:
-            fin[...] = x
+            arrive(third)
+            first = 1.2 * c1x[1:2] + wide[2:3] * sum_inner(c1x[0:3], lanes)
+            final = 1.2 * c1x[d + 4:d + 5] + wide[-3:-2] * sum_inner(c1x[d + 3:d + 6], lanes)
+            x = jnp.concatenate([first, x, final], 0) + lift
+            x = (0.2 * x[1:-1] + c1x[2:d + 4]) + a * sum_inner(x, lanes)
+            fin[...] = (0.2 * x[1:-1] + c1x[3:d + 3]) + a[1:-1] * sum_inner(x, lanes)
 
     onward = pltpu.make_async_remote_copy(
         fin, up_ref, ts.at[0], ts.at[1],
@@ -292,8 +363,10 @@
     def _():
         up_ref[...] = u0[...]
 
-    for pair in near + far + [cap_near, cap_far]:
+    for pair in (near, far, beyond, source, third, cap_near, cap_far):
         sent(pair)
+    for pair in (pass_near, pass_far):
+        each(pair, lambda copy: copy.wait_send())
     for copies in [gather_cap] + gather_r:
         for copy in copies:
             copy.wait_send()
@@ -311,6 +384,7 @@
     parts, spans = lax.axis_size("space"), lax.axis_size("tm")
     steps = source_power.shape[1]
     depth, rows, lanes = warmth_retention.shape
+    assert steps == 2 and depth == 4
     slab = jax.ShapeDtypeStruct((depth, rows, lanes), F32)
     vmem = pl.BlockSpec(memory_space=pltpu.VMEM)
     dma = pltpu.SemaphoreType.DMA
@@ -321,16 +395,18 @@
         out_specs=(vmem, vmem),
         scratch_shapes=[
             pltpu.VMEM((depth, rows, lanes), F32),
-            pltpu.VMEM((steps, depth, rows, lanes), F32),
+            pltpu.VMEM((depth, rows, lanes), F32),
             pltpu.VMEM((depth + 4, rows, lanes), F32),
-            pltpu.VMEM((steps, depth + 6, rows, lanes), F32),
+            pltpu.VMEM((3 * depth, rows, lanes), F32),
+            pltpu.VMEM((3 * depth + 2, rows, lanes), F32),
+            pltpu.VMEM((depth + 6, rows, lanes), F32),
             pltpu.VMEM((parts, rows // 2, lanes), F32),
             pltpu.VMEM((steps, parts, rows // 2, lanes), F32),
             pltpu.VMEM((depth, rows, lanes), F32),
             pltpu.VMEM((parts + 2, rows // 2, lanes), F32),
-            pltpu.VMEM((max(parts * rows // 2, (depth // 2 + 2) * rows), lanes), F32),
+            pltpu.VMEM((max(parts * rows // 2, 6 * rows), lanes), F32),
             pltpu.VMEM((depth, rows, lanes), F32),
-            dma((3,)), dma((4 * steps,)), dma((4 * steps,)), dma((4,)), dma((4,)),
+            dma((4,)), dma((10,)), dma((10,)), dma((4,)), dma((4,)), dma((4, spans)), dma((4, spans)),
             dma((1 + steps, parts)), dma((1 + steps, parts)), dma((2,)),
         ],
         compiler_params=pltpu.CompilerParams(

time: 39.3 us -> 36.1 us (0.919)
  Pallas kernels: 37.2 us -> 34 us
    pallas_call x1, Pallas kernels: 37.2 us -> 34 us  [shards(): pl.pallas_call(functools.partial(kernel, parts, spans, steps), out_shape=...]
where the time goes in v3:
time: 36.1 us; the launch traced here: 36 us
  Pallas kernels  34 us (94%)
  local copies, waits for them, and re-layouts  1.31 us (4%)
  between operations  0.64 us (2%)
    pallas_call x1, Pallas kernels, shards(): pl.pallas_call(functools.partial(kernel, parts, spans, steps), out_shape=...  34 us
    unnamed x2, local copies, waits for them, and re-layouts  1.31 us

profile of v3, /device:TPU:0, one launch (start us, length us, event | category | flops | bytes accessed | tf_op | source)
XLA Modules:
  0.0 36.0 jit_solution(9599104296885227343)
XLA Ops:
  0.6 34.0 %shard_map.50 = (f32[4,64,128]{2,1,0:T(8,128)S(1)}, f32[4,64,128]{2,1,0:T(8,128)S(1)}) custom-call(f32[4,64,128]{2,1,0:T(8,128)} %bitcast.7, f32[2,4,64,128]{3,2,1,0:T(8,128)} %bitcast.6, f32[4,64,128]{2,1,0:T(8,128)} %cap_in.1), custom_call_target="tpu_custom_call" | custom-call | tf_op jit(solution)/shard_map/pallas_call | solution.py:391
  34.7 0.7 %copy.7 = f32[1,4,64,128]{3,2,1,0:T(8,128)} copy(f32[1,4,64,128]{3,2,1,0:T(8,128)S(1)} %bitcast.5) | data formatting | bytes 262144
  35.3 0.7 %copy.8 = f32[1,4,64,128]{3,2,1,0:T(8,128)} copy(f32[1,4,64,128]{3,2,1,0:T(8,128)S(1)} %bitcast.4) | data formatting | bytes 262144

commit v4 on v3

--- a/solution.py
+++ b/solution.py
@@ -18,12 +18,18 @@
 
 
 def dot(a, b):
-    return jnp.dot(a, b, precision=lax.Precision.HIGHEST, preferred_element_type=F32)
+    total = None
+    for _ in range(3):
+        part = a.astype(jnp.bfloat16)
+        a = a - part.astype(F32)
+        term = jnp.dot(part, b, preferred_element_type=F32)
+        total = term if total is None else total + term
+    return total
 
 
 def picks(lanes, pick, scale):
     src, dst = iota((lanes, lanes), 0), iota((lanes, lanes), 1)
-    return jnp.where(pick(src, dst), scale, 0.0).astype(F32)
+    return jnp.where(pick(src, dst), scale, 0.0).astype(jnp.bfloat16)
 
 
 def in_plane(x, width):
@@ -56,6 +62,38 @@
 
 def sum_inner(x, width):
     return in_plane(x[1:-1], width) + (x[:-2] + x[2:])
+
+
+def column_sum(x):
+    rows = x.shape[1]
+    row = iota(x.shape, 1)
+    before, after = shifted(x)
+    up = jnp.where(row == 0, 0.0, pltpu.roll(x, 1, 1))
+    down = jnp.where(row == rows - 1, 0.0, pltpu.roll(x, rows - 1, 1))
+    return (before + after) + (up + down)
+
+
+def coarse_solve(c, a, lanes):
+    def moved(x):
+        return pltpu.roll(x, 1, 2), x, pltpu.roll(x, lanes - 1, 2)
+
+    cs, as_ = moved(c), moved(a)
+
+    def two_sweeps(_, y):
+        far = pltpu.roll(y, 2, 2), pltpu.roll(y, lanes - 2, 2)
+        near = moved(y)
+        sides = far[0] + y, near[0] + near[2], y + far[1]
+        once = [
+            (0.2 * y_at + c_at) + a_at * (side + column_sum(y_at))
+            for y_at, c_at, a_at, side in zip(near, cs, as_, sides)
+        ]
+        return (0.2 * once[1] + c) + a * ((once[0] + once[2]) + column_sum(once[1]))
+
+    left = COARSE_SWEEPS - 1
+    y = c
+    if left % 2:
+        y = 1.2 * c + a * sum_planes(c, lanes // 8)
+    return lax.fori_loop(0, left // 2, two_sweeps, y, unroll=True)
 
 
 def flat(x):
@@ -305,9 +343,7 @@
         if t == 0:
             arrive(cap_far)
             each(pass_far, lambda copy: copy.start())
-        y3 = lax.fori_loop(
-            0, COARSE_SWEEPS - 1,
-            lambda _, y: (0.2 * y + c3) + a3 * sum_planes(y, lanes // 8), c3, unroll=True)
+        y3 = coarse_solve(c3, a3, lanes)
         lift = twice_rows(dot(flat(y3), up_3), parts // 2)
         lift = jnp.broadcast_to(lift[:, None], (parts // 2, 2) + lift.shape[1:]).reshape(y2.shape)
         y2 = y2 + lift

time: 36.1 us -> 35.1 us (0.972)
  Pallas kernels: 34 us -> 33 us
    pallas_call x1, Pallas kernels: 34 us -> 33 us  [shards(): pl.pallas_call(functools.partial(kernel, parts, spans, steps), out_shape=...]
where the time goes in v4:
time: 35.1 us; the launch traced here: 35 us
  Pallas kernels  33 us (94%)
  local copies, waits for them, and re-layouts  1.31 us (4%)
  between operations  0.64 us (2%)
    pallas_call x1, Pallas kernels, shards(): pl.pallas_call(functools.partial(kernel, parts, spans, steps), out_shape=...  33 us
    unnamed x2, local copies, waits for them, and re-layouts  1.31 us

profile of v4, /device:TPU:0, one launch (start us, length us, event | category | flops | bytes accessed | tf_op | source)
XLA Modules:
  0.0 35.0 jit_solution(676834959445002394)
XLA Ops:
  0.6 33.0 %shard_map.50 = (f32[4,64,128]{2,1,0:T(8,128)S(1)}, f32[4,64,128]{2,1,0:T(8,128)S(1)}) custom-call(f32[4,64,128]{2,1,0:T(8,128)} %bitcast.7, f32[2,4,64,128]{3,2,1,0:T(8,128)} %bitcast.6, f32[4,64,128]{2,1,0:T(8,128)} %cap_in.1), custom_call_target="tpu_custom_call" | custom-call | tf_op jit(solution)/shard_map/pallas_call | solution.py:427
  33.7 0.7 %copy.7 = f32[1,4,64,128]{3,2,1,0:T(8,128)} copy(f32[1,4,64,128]{3,2,1,0:T(8,128)S(1)} %bitcast.5) | data formatting | bytes 262144
  34.3 0.7 %copy.8 = f32[1,4,64,128]{3,2,1,0:T(8,128)} copy(f32[1,4,64,128]{3,2,1,0:T(8,128)S(1)} %bitcast.4) | data formatting | bytes 262144

commit v5 on v4

--- a/solution.py
+++ b/solution.py
@@ -274,20 +274,19 @@
     x1p[parts + 1] = jnp.zeros(x1p.shape[1:], F32)
 
     loads[0].wait()
+    pl.semaphore_wait(barrier, parts - 1 + spans - 1)
+    begin(cap_near)
     mine = cap[d:2 * d]
-    gcap[me] = pack(mine)
     loads[1].wait()
     loads[2].wait()
     b = mine * u0[...] + src0[...]
     own[...] = b
     c0[d + 1:2 * d + 1] = b * (W / (mine + 6.0))
-    loads[3].wait()
-
-    pl.semaphore_wait(barrier, parts - 1 + spans - 1)
-    begin(cap_near)
     begin(near)
+    gcap[me] = pack(mine)
     for copy in gather_cap:
         copy.start()
+    loads[3].wait()
 
     def weights(start, count):
         plane = (me - 1) * depth + start + iota((count, 1, 1), 0)

time: 35.1 us -> 35 us (level)
  no operation moved by 1% of the time
where the time goes in v5:
time: 35 us; the launch traced here: 34.8 us
  Pallas kernels  32.9 us (94%)
  local copies, waits for them, and re-layouts  1.31 us (4%)
  between operations  0.64 us (2%)
    pallas_call x1, Pallas kernels, shards(): pl.pallas_call(functools.partial(kernel, parts, spans, steps), out_shape=...  32.9 us
    unnamed x2, local copies, waits for them, and re-layouts  1.31 us

profile of v5, /device:TPU:0, one launch (start us, length us, event | category | flops | bytes accessed | tf_op | source)
XLA Modules:
  0.0 34.8 jit_solution(17276821832499871723)
XLA Ops:
  0.6 32.9 %shard_map.50 = (f32[4,64,128]{2,1,0:T(8,128)S(1)}, f32[4,64,128]{2,1,0:T(8,128)S(1)}) custom-call(f32[4,64,128]{2,1,0:T(8,128)} %bitcast.7, f32[2,4,64,128]{3,2,1,0:T(8,128)} %bitcast.6, f32[4,64,128]{2,1,0:T(8,128)} %cap_in.1), custom_call_target="tpu_custom_call" | custom-call | tf_op jit(solution)/shard_map/pallas_call | solution.py:426
  33.5 0.7 %copy.7 = f32[1,4,64,128]{3,2,1,0:T(8,128)} copy(f32[1,4,64,128]{3,2,1,0:T(8,128)S(1)} %bitcast.5) | data formatting | bytes 262144
  34.2 0.7 %copy.8 = f32[1,4,64,128]{3,2,1,0:T(8,128)} copy(f32[1,4,64,128]{3,2,1,0:T(8,128)S(1)} %bitcast.4) | data formatting | bytes 262144
